TPU v7x, 32 devices: a whole 2x2x4 slice. The times are simulated.
32 devices in a mesh: grp: 8 (over y, x, core), sub: 4 (over z).
Axes of the slice: x: 2, y: 2, z: 4, core: 2. Of those that a mesh axis runs over, the one named last changes fastest.
Arguments:
- master: float32 [4096, 3584], P(('grp', 'sub')), may hold values from -120 to 120
- moment_one: float32 [4096, 3584], P(('grp', 'sub')), may hold values from -6 to 6
- moment_two: float32 [4096, 3584], P(('grp', 'sub')), may hold values from 0.01 to 4
- gradient: float32 [4096, 3584], P(('grp', 'sub')), may hold values from -120 to 120
- partner: int32 [32], replicated, may hold values from 0 to 31, each once
- tensor_of_row: int32 [4096], replicated, may hold values from 0 to 7, never falling along the last dimension, each value on 1 to 1024 neighbouring positions
Outputs:
- new_master: float32 [4096, 3584], P(('grp', 'sub'))
- new_moment_one: float32 [4096, 3584], P(('grp', 'sub'))
- new_moment_two: float32 [4096, 3584], P(('grp', 'sub'))
Inputs may be any that keep to these rules, and one draw needn't show every extreme that they name: partner[n] is the device of new rank n; every device holds exactly one rank. `tensor_of_row`: tensor numbers never fall along the rows; each of the 8 tensors has one or more rows.
All inputs are finite; a program needn't handle non-finite values.
Results may differ from a plain program's by a relative error of at most 0.00007.
Values sent between devices are 32-bit elements; how exact they have to be, the bound alone decides.
A program may use at most 128 MiB of HBM per device.

v0:
```python
import jax
import jax.numpy as jnp
from jax import lax
from jax.sharding import PartitionSpec as P

LAYERS = 8


beta_one = 0.9
beta_two = 0.999
step_count = 10
adam_eps = 1e-06
trust_eps = 1e-06
learn_rate = 0.05
decay_rate = 0.01


def tensor_totals(values, onehot):
    return jnp.dot(values[None, :], onehot, precision=lax.Precision.HIGHEST)[0]


def local(master, moment_one, moment_two, gradient, partner, tensor_of_row):
    rows_dev, width = master.shape
    devices = lax.axis_size(("grp", "sub"))
    block = rows_dev // devices
    device_id = lax.axis_index(("grp", "sub"))
    numbers = jnp.arange(devices, dtype=jnp.int32)
    matches = partner[None, :] == numbers[:, None]
    inverse = jnp.sum(jnp.where(matches, numbers[None, :], 0), axis=1)
    my_rank = lax.dynamic_index_in_dim(inverse, device_id, 0, keepdims=False)
    layer_ids = jnp.arange(LAYERS, dtype=jnp.int32)
    id_grid = tensor_of_row.reshape(devices, devices, block)
    new_ids = lax.dynamic_index_in_dim(id_grid, my_rank, 1, keepdims=False).reshape(rows_dev)
    new_hot = (new_ids[:, None] == layer_ids[None, :]).astype(jnp.float32)
    old_ids = lax.dynamic_slice_in_dim(tensor_of_row, device_id * rows_dev, rows_dev)
    old_hot = (old_ids[:, None] == layer_ids[None, :]).astype(jnp.float32)
    weight_sq = lax.psum(tensor_totals(jnp.sum(master * master, axis=1), old_hot), ("grp", "sub"))

    def outbound(values):
        return jnp.take(values.reshape(devices, block, width), inverse, axis=0)

    sending = (outbound(master), outbound(moment_one), outbound(moment_two))
    arrived = (
        lax.all_to_all(sending[0], ("grp", "sub"), split_axis=0, concat_axis=0, tiled=True),
        lax.all_to_all(sending[1], ("grp", "sub"), split_axis=0, concat_axis=0, tiled=True),
        lax.all_to_all(sending[2], ("grp", "sub"), split_axis=0, concat_axis=0, tiled=True),
    )
    weights, moment_old, square_old = [piece.reshape(rows_dev, width) for piece in arrived]
    first = beta_one * moment_old + (1.0 - beta_one) * gradient
    second = beta_two * square_old + (1.0 - beta_two) * gradient * gradient
    correct_one = 1.0 - beta_one**step_count
    correct_two = 1.0 - beta_two**step_count
    update = (
        first / correct_one / (jnp.sqrt(second / correct_two) + adam_eps) + decay_rate * weights
    )
    update_local = tensor_totals(jnp.sum(update * update, axis=1), new_hot)
    update_sq = lax.psum(update_local, ("grp", "sub"))
    ratio = jnp.sqrt(weight_sq) / (jnp.sqrt(update_sq) + trust_eps)
    row_ratio = jnp.dot(new_hot, ratio[:, None], precision=lax.Precision.HIGHEST)
    fresh = weights - learn_rate * row_ratio * update
    return (fresh, first, second)


def solution(mesh):
    return jax.shard_map(
        local,
        mesh=mesh,
        in_specs=(
            P(("grp", "sub"), None),
            P(("grp", "sub"), None),
            P(("grp", "sub"), None),
            P(("grp", "sub"), None),
            P(),
            P(),
        ),
        out_specs=(P(("grp", "sub"), None), P(("grp", "sub"), None), P(("grp", "sub"), None)),
        check_vma=False,
    )
```

profile of v0, /device:TPU:0, one launch (start us, length us, event | category | flops | bytes accessed | tf_op | source)
XLA Modules:
  0.0 219.0 jit_solution(205470790843580463)
XLA Ops:
  0.6 0.8 select_reduce_fusion
  1.4 1.9 reshape.52
  3.3 2.8 %reshape.53 = f32[32,4,3584]{2,1,0:T(4,128)} reshape(f32[128,3584]{1,0:T(8,128)} %param.10) | data formatting | bytes 3670016 | tf_op jit(solution)/shard_map/reshape | solution.py:40
  6.2 2.8 %gather_fusion.1 = f32[32,4,3584]{2,1,0:T(4,128)} fusion(f32[32,4,3584]{2,1,0:T(4,128)S(1)} %reshape.52, s32[1024]{0:T(1024)S(1)} %pad_clamp_fusion), kind=kCustom, calls=%fused_computation.1.clone | custom fusion | bytes 3670144 | tf_op jit(solution)/shard_map/jit(_take)/gather | solution.py:40
  8.9 4.4 %gather_fusion.2 = f32[32,4,3584]{2,1,0:T(4,128)} fusion(f32[32,4,3584]{2,1,0:T(4,128)} %reshape.53, s32[1024]{0:T(1024)S(1)} %pad_clamp_fusion), kind=kCustom, calls=%fused_computation.2.clone | custom fusion | bytes 3670144 | tf_op jit(solution)/shard_map/jit(_take)/gather | solution.py:40
  13.3 0.0 copy-done.1
  13.3 1.8 reshape.49
  15.1 4.4 %gather_fusion = f32[32,4,3584]{2,1,0:T(4,128)} fusion(f32[32,4,3584]{2,1,0:T(4,128)} %reshape.49, s32[1024]{0:T(1024)S(1)} %pad_clamp_fusion), kind=kCustom, calls=%fused_computation.clone | custom fusion | bytes 3670144 | tf_op jit(solution)/shard_map/jit(_take)/gather | solution.py:40
  19.5 4.6 %broadcast_select_fusion = (f32[32,4,3584]{2,1,0:T(4,128)S(1)}, f32[32,4,3584]{2,1,0:T(4,128)S(1)}, f32[32,4,3584]{2,1,0:T(4,128)}) fusion(f32[32,4,3584]{2,1,0:T(4,128)} %gather_fusion.2, pred[32]{0:T(512)(128)(4,1)S(1)} %compare_and_fusion, f32[32,4,3584]{2,1,0:T(4,128)S(1)} %copy-done.2, f32[32,4,3584]{2,1,0:T(4,128)} %gather_fusion), kind=kLoop, calls=%fused_computation.14 | loop fusion | flops 1376256 | bytes 11010080 | tf_op jit(solution)/shard_map/jit(_take)/select_n | solution.py:40
  24.1 49.2 %all_to_all.15 = f32[32,4,3584]{2,1,0:T(4,128)} all-to-all(f32[32,4,3584]{2,1,0:T(4,128)S(1)} %get-tuple-element.9), channel_id=1, replica_groups=mesh['grp'=8,'sub'=4] {'grp','sub'}, dimensions={0} | all-to-all | bytes 3670016 | tf_op jit(solution)/shard_map/all_to_all | solution.py:46
  73.3 46.2 %all_to_all.16 = f32[32,4,3584]{2,1,0:T(4,128)S(1)} all-to-all(f32[32,4,3584]{2,1,0:T(4,128)S(1)} %get-tuple-element.10), channel_id=1, replica_groups=mesh['grp'=8,'sub'=4] {'grp','sub'}, dimensions={0} | all-to-all | bytes 3670016 | tf_op jit(solution)/shard_map/all_to_all | solution.py:45
  119.5 4.8 %all-to-all-start = ((f32[32,4,3584]{2,1,0:T(4,128)}), f32[32,4,3584]{2,1,0:T(4,128)}, u32[]{:S(2)}, u32[]{:S(2)}) async-start(f32[32,4,3584]{2,1,0:T(4,128)} %get-tuple-element.11), calls=%async_computation | async-start | bytes 3670016 | tf_op jit(solution)/shard_map/all_to_all | solution.py:44
  124.3 0.6 dynamic_slice.11
  126.2 0.5 reshape.51
  126.7 0.1 dynamic_slice.13
  127.5 0.1 dynamic-slice_reduce_fusion
  127.5 0.1 eq.44
  127.6 0.0 copy-start
  127.7 1.8 multiply_reduce_fusion.1
  129.5 0.2 convolution_bitcast_fusion.2
  129.7 0.0 copy-done
  129.7 1.7 broadcast_multiply_fusion
  131.4 2.9 %mul.76 = f32[128,3584]{1,0:T(8,128)} reshape(f32[32,4,3584]{2,1,0:T(4,128)} %broadcast_multiply_fusion) | data formatting | bytes 3670016 | tf_op jit(solution)/shard_map/mul | solution.py:50
  134.3 1.7 broadcast_multiply_fusion.1
  136.0 2.9 %mul.71 = f32[128,3584]{1,0:T(8,128)} reshape(f32[32,4,3584]{2,1,0:T(4,128)} %broadcast_multiply_fusion.1) | data formatting | bytes 3670016 | tf_op jit(solution)/shard_map/mul | solution.py:49
  138.9 26.5 %all-to-all-done = f32[32,4,3584]{2,1,0:T(4,128)} async-done(((f32[32,4,3584]{2,1,0:T(4,128)}), f32[32,4,3584]{2,1,0:T(4,128)}, u32[]{:S(2)}, u32[]{:S(2)}) %all-to-all-start) | async-done | bytes 1835040 | tf_op jit(solution)/shard_map/all_to_all | solution.py:44
  165.4 1.9 reshape.50
  167.3 5.7 %multiply_reduce_fusion = (f32[128]{0:T(128)S(1)}, f32[128,3584]{1,0:T(8,128)}, f32[128,3584]{1,0:T(8,128)}) fusion(f32[128,3584]{1,0:T(8,128)S(1)} %reshape.50, f32[128,3584]{1,0:T(8,128)} %mul.71, f32[128,3584]{1,0:T(8,128)} %param.11, f32[128,3584]{1,0:T(8,128)} %mul.76), kind=kLoop, calls=%fused_computation.6 | loop fusion | flops 5963648 | bytes 11010560 | tf_op jit(solution)/shard_map/reduce_sum | solution.py:56
  173.0 0.2 convolution_bitcast_fusion.1
  173.2 41.3 %all-reduce = (f32[8]{0:T(128)S(1)}, f32[8]{0:T(128)S(1)}) all-reduce(f32[8]{0:T(128)S(1)} %convolution_bitcast_fusion.1, f32[8]{0:T(128)S(1)} %convolution_bitcast_fusion.2), channel_id=1, replica_groups=mesh['grp'=8,'sub'=4] {'grp','sub'}, use_global_device_ids=true, to_apply=%region_4.6 | all-reduce | flops 16 | bytes 128 | tf_op jit(solution)/shard_map/psum | solution.py:57
  214.5 0.2 fusion.1
  214.7 4.3 %multiply_subtract_fusion = f32[128,3584]{1,0:T(8,128)} fusion(f32[128,3584]{1,0:T(8,128)S(1)} %reshape.50, f32[128]{0:T(128)S(1)} %fusion.1, f32[128,3584]{1,0:T(8,128)} %get-tuple-element.8, f32[128,3584]{1,0:T(8,128)} %get-tuple-element.7), kind=kLoop, calls=%fused_computation.5 | loop fusion | flops 3670016 | bytes 7340544 | tf_op jit(solution)/shard_map/sub | solution.py:60
  (8 shorter events, 0.0 us)
Async XLA Ops:
  8.9 4.4 %copy-start.1 = (f32[128,3584]{1,0:T(8,128)S(1)}, f32[128,3584]{1,0:T(8,128)}, u32[]{:S(2)}) copy-start(f32[128,3584]{1,0:T(8,128)} %param.8) | copy-start | bytes 5505028
  15.1 4.4 %copy-start.2 = (f32[32,4,3584]{2,1,0:T(4,128)S(1)}, f32[32,4,3584]{2,1,0:T(4,128)}, u32[]{:S(2)}) copy-start(f32[32,4,3584]{2,1,0:T(4,128)} %gather_fusion.1) | copy-start | bytes 5505028
  119.5 6.7 %copy-start.3 = (s32[4096]{0:T(1024)S(1)}, s32[4096]{0:T(1024)}, u32[]{:S(2)}) copy-start(s32[4096]{0:T(1024)} %param.13) | copy-start | bytes 49156
  119.5 45.8 %all-to-all-start = ((f32[32,4,3584]{2,1,0:T(4,128)}), f32[32,4,3584]{2,1,0:T(4,128)}, u32[]{:S(2)}, u32[]{:S(2)}) async-start(f32[32,4,3584]{2,1,0:T(4,128)} %get-tuple-element.11), calls=%async_computation | async-start | bytes 3670016 | tf_op jit(solution)/shard_map/all_to_all | solution.py:44
  127.6 2.1 copy-start
where the time goes:
time: 219 us
  blocking collectives  137 us (63%)
  local copies, waits for them, and re-layouts  27.1 us (12%)
  waiting for transfers between devices  26.5 us (12%)
  other arithmetic  20.7 us (9%)
  starting transfers between devices  4.76 us (2%)
  between operations  2.68 us (1%)
    all_to_all x1, blocking collectives, local(): lax.all_to_all(sending[2], ('grp', 'sub'), split_axis=0, concat_axis=0, t...  49.2 us
    all_to_all x1, blocking collectives, local(): lax.all_to_all(sending[1], ('grp', 'sub'), split_axis=0, concat_axis=0, t...  46.2 us
    psum x1, blocking collectives, local(): update_sq = lax.psum(update_local, ('grp', 'sub'))  41.3 us
    all_to_all x1, waiting for transfers between devices, local(): lax.all_to_all(sending[0], ('grp', 'sub'), split_axis=0, concat_axis=0, t...  26.5 us
    gather x3, local copies, waits for them, and re-layouts, outbound(): return jnp.take(values.reshape(devices, block, width), inverse, axis=0)  11.6 us
    reshape x3, local copies, waits for them, and re-layouts, outbound(): return jnp.take(values.reshape(devices, block, width), inverse, axis=0)  6.49 us
    reduce_sum x1, other arithmetic, local(): update_local = tensor_totals(jnp.sum(update * update, axis=1), new_hot)  5.68 us
    all_to_all x1, starting transfers between devices, local(): lax.all_to_all(sending[0], ('grp', 'sub'), split_axis=0, concat_axis=0, t...  4.76 us
  transfers between devices with their start and end apart: 1, of which 1 were waited for; matrix products, arithmetic and copies ran while one was open for 6% of the time, Pallas kernels for 0%

commit v1 on v0

v1 whole, which is shorter than its diff:
```python
import functools

import jax
import jax.numpy as jnp
from jax import lax
from jax.experimental import pallas as pl
from jax.experimental.pallas import tpu as pltpu
from jax.sharding import PartitionSpec as P

LAYERS = 8
LANES = 128
TILE = 8
MESH = pl.DeviceIdType.MESH

beta_one = 0.9
beta_two = 0.999
step_count = 10
adam_eps = 1e-06
trust_eps = 1e-06
learn_rate = 0.05
decay_rate = 0.01


def xor(a, b, bound):
    total, bit = 0, 1
    while bit < bound:
        total = total + ((a // bit + b // bit) % 2) * bit
        bit *= 2
    return total


def prepare(groups, subs, partner, ids, master_hbm, one_hbm, two_hbm, staged, row_ids,
            master, one, two, load_sem):
    devices = groups * subs
    rows_dev, width = master.shape
    block = rows_dev // devices
    many = TILE // block
    me = lax.axis_index("grp") * subs + lax.axis_index("sub")
    loads = [
        pltpu.make_async_copy(src, dst, load_sem.at[i])
        for i, (src, dst) in enumerate([(master_hbm, master), (one_hbm, one), (two_hbm, two)])
    ]
    for load in loads:
        load.start()

    def rank_of(device):
        def seek(n, found):
            return found + jnp.where(partner[n] == device, n, 0)

        return lax.fori_loop(0, devices, seek, jnp.int32(0), unroll=8)

    my_rank = rank_of(me)
    sub_iota = lax.broadcasted_iota(jnp.int32, (TILE, LANES), 0)

    def name_rows(s, carry):
        here = jnp.zeros((TILE, LANES), jnp.int32)
        for i in range(many):
            for b in range(block):
                tensor = ids[(s * many + i) * rows_dev + my_rank * block + b]
                here = jnp.where(sub_iota == i * block + b, tensor, here)
        row_ids[pl.ds(pl.multiple_of(s * TILE, TILE), TILE), :] = here
        return carry

    lax.fori_loop(0, rows_dev // TILE, name_rows, 0)
    for load in loads:
        load.wait()

    def stage(n, carry):
        peer = partner[n]
        base = pl.multiple_of((n // many) * TILE, TILE)
        part = n % many
        for a, source in enumerate((master, one, two)):
            rows = source[pl.ds(base, TILE), :]
            piece = rows[:block]
            for i in range(1, many):
                piece = jnp.where(part == i, rows[i * block : (i + 1) * block], piece)
            staged[peer, a] = piece
        return carry

    lax.fori_loop(0, devices, stage, 0)


def kernel(groups, subs, staged, row_ids, grad_hbm,
           fresh, first_out, second_out,
           grad, landed, update, acc_w, acc_u, sums,
           load_sem, send_sem, recv_sem, sum_send, sum_recv):
    devices = groups * subs
    rows_dev, width = grad.shape
    block = rows_dev // devices
    many = TILE // block
    tiles = rows_dev // TILE
    columns = width // LANES
    me = lax.axis_index("grp") * subs + lax.axis_index("sub")

    def at(peer):
        return {"grp": peer // subs, "sub": peer % subs}

    load = pltpu.make_async_copy(grad_hbm, grad, load_sem)
    load.start()
    barrier = pltpu.get_barrier_semaphore()

    def greet(k, carry):
        pl.semaphore_signal(barrier, inc=1, device_id=at(xor(me, k, devices)), device_id_type=MESH)
        return carry

    lax.fori_loop(1, devices, greet, 0)
    pl.semaphore_wait(barrier, devices - 1)

    def tile_at(s):
        halves = subs // many
        return (groups - 1 - s % groups) * halves + (halves - 1 - s // groups)

    def peer_at(t):
        return tile_at(t // many) * many + (many - 1 - t % many)

    def exchange(k):
        return pltpu.make_async_remote_copy(
            src_ref=staged.at[xor(me, k, devices)],
            dst_ref=landed.at[k],
            send_sem=send_sem.at[k],
            recv_sem=recv_sem.at[k],
            device_id=at(xor(me, k, devices)),
            device_id_type=MESH,
        )

    def send(t, carry):
        exchange(peer_at(t)).start()
        return carry

    lax.fori_loop(0, devices - 1, send, 0)
    landed[0] = staged[me]
    load.wait()
    acc_w[...] = jnp.zeros_like(acc_w)
    acc_u[...] = jnp.zeros_like(acc_u)
    sub_iota = lax.broadcasted_iota(jnp.int32, (TILE, LANES), 0)
    lane_iota = lax.broadcasted_iota(jnp.int32, (TILE, LANES), 1)
    scale_one = 1.0 / (1.0 - beta_one**step_count)
    scale_two = 1.0 / (1.0 - beta_two**step_count)

    def consume(j):
        first_owner = xor(me // many, j, devices // many) * many
        base = pl.multiple_of(first_owner * block, TILE)
        slots = [j * many + xor(me % many, i, many) for i in range(many)]
        here = row_ids[pl.ds(base, TILE), :]
        sum_w = jnp.zeros((TILE, LANES), jnp.float32)
        sum_u = jnp.zeros((TILE, LANES), jnp.float32)
        for c in range(columns):
            cut = slice(c * LANES, (c + 1) * LANES)

            def arrived(a):
                return jnp.concatenate([landed[slot, a, :, cut] for slot in slots], axis=0)

            g = grad[pl.ds(base, TILE), cut]
            w = arrived(0)
            first = beta_one * arrived(1) + (1.0 - beta_one) * g
            second = beta_two * arrived(2) + (1.0 - beta_two) * g * g
            u = (first * scale_one) / (jnp.sqrt(second * scale_two) + adam_eps) + decay_rate * w
            first_out[pl.ds(base, TILE), cut] = first
            second_out[pl.ds(base, TILE), cut] = second
            fresh[pl.ds(base, TILE), cut] = w
            update[pl.ds(base, TILE), cut] = u
            sum_w += w * w
            sum_u += u * u
        for t in range(LAYERS):
            acc_w[t] += jnp.where(here == t, sum_w, 0.0)
            acc_u[t] += jnp.where(here == t, sum_u, 0.0)

    def receive(s, carry):
        j = tile_at(s)
        for i in range(many):
            exchange(j * many + i).wait_recv()
        consume(j)
        return carry

    lax.fori_loop(0, tiles - 1, receive, 0)
    for i in range(1, many):
        exchange(i).wait_recv()
    consume(0)

    col_w = jnp.sum(jnp.sum(acc_w[...], axis=1), axis=1, keepdims=True)
    col_u = jnp.sum(jnp.sum(acc_u[...], axis=1), axis=1, keepdims=True)
    spread = jnp.where(lane_iota == sub_iota, col_w, 0.0) + jnp.where(
        lane_iota == sub_iota + LAYERS, col_u, 0.0
    )
    sums[0] = jnp.sum(spread, axis=0, keepdims=True)

    def exchange_sum(k):
        return pltpu.make_async_remote_copy(
            src_ref=sums.at[0],
            dst_ref=sums.at[k],
            send_sem=sum_send.at[k],
            recv_sem=sum_recv.at[k],
            device_id=at(xor(me, k, devices)),
            device_id_type=MESH,
        )

    def send_sum(t, carry):
        exchange_sum(devices - 1 - t).start()
        return carry

    lax.fori_loop(0, devices - 1, send_sum, 0)

    def drain(k, carry):
        exchange(k).wait_send()
        return carry

    lax.fori_loop(1, devices, drain, 0)

    def drain_sum(k, carry):
        exchange_sum(k).wait_recv()
        exchange_sum(k).wait_send()
        return carry

    lax.fori_loop(1, devices, drain_sum, 0)

    def gather_sum(o, total):
        return total + sums[xor(me, o, devices)]

    total = lax.fori_loop(0, devices, gather_sum, jnp.zeros((1, LANES), jnp.float32), unroll=8)
    wide = jnp.broadcast_to(total, (TILE, LANES))
    weight_sq = jnp.sum(jnp.where(lane_iota == sub_iota, wide, 0.0), axis=1, keepdims=True)
    update_sq = jnp.sum(jnp.where(lane_iota == sub_iota + LAYERS, wide, 0.0), axis=1, keepdims=True)
    ratio = learn_rate * (jnp.sqrt(weight_sq) / (jnp.sqrt(update_sq) + trust_eps))
    ratio = jnp.broadcast_to(ratio, (TILE, LANES))

    def finish(s, carry):
        base = pl.multiple_of(s * TILE, TILE)
        here = row_ids[pl.ds(base, TILE), :]
        step = jnp.zeros((TILE, LANES), jnp.float32)
        for t in range(LAYERS):
            step = jnp.where(here == t, jnp.broadcast_to(ratio[t : t + 1], (TILE, LANES)), step)
        for c in range(columns):
            cut = slice(c * LANES, (c + 1) * LANES)
            fresh[pl.ds(base, TILE), cut] -= step * update[pl.ds(base, TILE), cut]
        return carry

    lax.fori_loop(0, tiles, finish, 0)


def local(groups, subs, master, moment_one, moment_two, gradient, partner, tensor_of_row):
    rows_dev, width = master.shape
    devices = groups * subs
    block = rows_dev // devices
    whole = jax.ShapeDtypeStruct((rows_dev, width), jnp.float32)
    vmem = pl.BlockSpec(memory_space=pltpu.VMEM)
    smem = pl.BlockSpec(memory_space=pltpu.SMEM)
    hbm = pl.BlockSpec(memory_space=pl.ANY)
    slots = (devices, 3, block, width)
    staged, row_ids = pl.pallas_call(
        functools.partial(prepare, groups, subs),
        out_shape=(
            jax.ShapeDtypeStruct(slots, jnp.float32),
            jax.ShapeDtypeStruct((rows_dev, LANES), jnp.int32),
        ),
        in_specs=[smem, smem, hbm, hbm, hbm],
        out_specs=(vmem, vmem),
        scratch_shapes=[pltpu.VMEM((rows_dev, width), jnp.float32)] * 3
        + [pltpu.SemaphoreType.DMA((3,))],
        compiler_params=pltpu.CompilerParams(vmem_limit_bytes=32 * 1024 * 1024),
    )(partner, tensor_of_row, master, moment_one, moment_two)
    return pl.pallas_call(
        functools.partial(kernel, groups, subs),
        out_shape=(whole, whole, whole),
        in_specs=[vmem, vmem, hbm],
        out_specs=(vmem, vmem, vmem),
        scratch_shapes=[
            pltpu.VMEM((rows_dev, width), jnp.float32),
            pltpu.VMEM(slots, jnp.float32),
            pltpu.VMEM((rows_dev, width), jnp.float32),
            pltpu.VMEM((LAYERS, TILE, LANES), jnp.float32),
            pltpu.VMEM((LAYERS, TILE, LANES), jnp.float32),
            pltpu.VMEM((devices, 1, LANES), jnp.float32),
            pltpu.SemaphoreType.DMA,
            pltpu.SemaphoreType.DMA((devices,)),
            pltpu.SemaphoreType.DMA((devices,)),
            pltpu.SemaphoreType.DMA((devices,)),
            pltpu.SemaphoreType.DMA((devices,)),
        ],
        compiler_params=pltpu.CompilerParams(
            collective_id=0, has_side_effects=True, vmem_limit_bytes=40 * 1024 * 1024
        ),
    )(staged, row_ids, gradient)


def solution(mesh):
    rows = P(("grp", "sub"), None)
    return jax.shard_map(
        functools.partial(local, mesh.shape["grp"], mesh.shape["sub"]),
        mesh=mesh,
        in_specs=(rows, rows, rows, rows, P(), P()),
        out_specs=(rows, rows, rows),
        check_vma=False,
    )
```

time: 219 us -> 158 us (0.72)
  Pallas kernels: 0 us -> 147 us
  blocking collectives: 137 us -> 0 us
  waiting for transfers between devices: 26.5 us -> 0 us
  other arithmetic: 20.7 us -> 0 us
  local copies, waits for them, and re-layouts: 27.1 us -> 9.69 us
  starting transfers between devices: 4.76 us -> 0 us
    pallas_call x0 -> x2, Pallas kernels: none -> 147 us  [the longest x1 145 us: local(): pl.pallas_call(functools.partial(kernel, groups, subs), out_shape=(whole,...]
    all_to_all x2 -> x0, blocking collectives: 95.4 us -> none  [the longest x1 49.2 us: local(): lax.all_to_all(sending[2], ('grp', 'sub'), split_axis=0, concat_axis=0, t...]
    psum x1 -> x0, blocking collectives: 41.3 us -> none  [local(): update_sq = lax.psum(update_local, ('grp', 'sub'))]
    all_to_all x1 -> x0, waiting for transfers between devices: 26.5 us -> none  [local(): lax.all_to_all(sending[0], ('grp', 'sub'), split_axis=0, concat_axis=0, t...]
    gather x3 -> x0, local copies, waits for them, and re-layouts: 11.6 us -> none  [outbound(): return jnp.take(values.reshape(devices, block, width), inverse, axis=0)]
    unnamed x8 -> x15, local copies, waits for them, and re-layouts: 0.02 us -> 9.69 us
    reshape x5 -> x0, local copies, waits for them, and re-layouts: 8.96 us -> none  [the longest x3 6.49 us: outbound(): return jnp.take(values.reshape(devices, block, width), inverse, axis=0)]
    reduce_sum x3 -> x0, other arithmetic: 8.29 us -> none  [the longest x1 5.68 us: local(): update_local = tensor_totals(jnp.sum(update * update, axis=1), new_hot)]
  transfers between devices with their start and end apart: 1 -> 0, of which waited for: 1 -> 0; matrix products, arithmetic and copies ran while one was open for 6% -> 0% of each run, Pallas kernels for 0% -> 0%
where the time goes in v1:
time: 158 us
  Pallas kernels  147 us (93%)
  local copies, waits for them, and re-layouts  9.69 us (6%)
    pallas_call x1, Pallas kernels, local(): pl.pallas_call(functools.partial(kernel, groups, subs), out_shape=(whole,...  145 us
    unnamed x15, local copies, waits for them, and re-layouts  9.69 us

profile of v1, /device:TPU:0, one launch (start us, length us, event | category | flops | bytes accessed | tf_op | source)
XLA Modules:
  0.0 157.6 jit_solution(2475895357865483885)
XLA Ops:
  0.6 0.0 copy-start
  0.6 0.0 copy-start.1
  0.7 1.6 %copy-done.1 = f32[128,3584]{1,0:T(8,128)S(1)} copy-done((f32[128,3584]{1,0:T(8,128)S(1)}, f32[128,3584]{1,0:T(8,128)}, u32[]{:S(2)}) %copy-start.1) | copy-done | bytes 1835032
  2.3 0.0 copy-start.2
  2.3 1.5 copy-done.2
  3.8 0.0 copy-start.3
  3.8 1.5 copy-done.3
  5.3 0.0 copy-start.4
  5.3 0.7 copy-done.4
  6.0 0.0 copy-start.5
  6.0 0.7 copy-done.5
  6.6 2.7 %shard_map.85 = (f32[32,3,4,3584]{3,2,1,0:T(4,128)S(1)}, s32[128,128]{1,0:T(8,128)S(1)}) custom-call(s32[32]{0:T(128)S(1)} %copy-done.5, s32[4096]{0:T(1024)S(1)} %copy-done.4, f32[128,3584]{1,0:T(8,128)S(1)} %copy-done.1, f32[128,3584]{1,0:T(8,128)S(1)} %copy-done.2, f32[128,3584]{1,0:T(8,128)S(1)} %copy-done.3), custom_call_target="tpu_custom_call" | custom-call | tf_op jit(solution)/shard_map/pallas_call | solution.py:249
  9.4 0.0 copy-done
  9.4 144.6 %shard_map.86 = (f32[128,3584]{1,0:T(8,128)S(1)}, f32[128,3584]{1,0:T(8,128)S(1)}, f32[128,3584]{1,0:T(8,128)S(1)}) custom-call(f32[32,3,4,3584]{3,2,1,0:T(4,128)S(1)} %get-tuple-element.5.staged, s32[128,128]{1,0:T(8,128)S(1)} %get-tuple-element.6.row_ids, f32[128,3584]{1,0:T(8,128)S(1)} %copy-done), custom_call_target="tpu_custom_call" | custom-call | tf_op jit(solution)/shard_map/pallas_call | solution.py:261
  153.9 1.2 copy.12
  155.2 1.2 copy.13
  156.4 1.2 copy.14
Async XLA Ops:
  0.6 8.7 %copy-start = (f32[128,3584]{1,0:T(8,128)S(1)}, f32[128,3584]{1,0:T(8,128)}, u32[]{:S(2)}) copy-start(f32[128,3584]{1,0:T(8,128)} %grad_hbm.1) | copy-start | bytes 5505028
  0.6 1.6 %copy-start.1 = (f32[128,3584]{1,0:T(8,128)S(1)}, f32[128,3584]{1,0:T(8,128)}, u32[]{:S(2)}) copy-start(f32[128,3584]{1,0:T(8,128)} %master_hbm.1) | copy-start | bytes 5505028
  2.3 1.5 copy-start.2
  3.8 1.5 copy-start.3
  5.3 0.7 copy-start.4
  6.0 0.7 copy-start.5

commit v2 on v1

v2 whole, which is shorter than its diff:
```python
import functools

import jax
import jax.numpy as jnp
from jax import lax
from jax.experimental import pallas as pl
from jax.experimental.pallas import tpu as pltpu
from jax.sharding import PartitionSpec as P

LAYERS = 8
LANES = 128
TILE = 8
PIECES = 4
MESH = pl.DeviceIdType.MESH

beta_one = 0.9
beta_two = 0.999
step_count = 10
adam_eps = 1e-06
trust_eps = 1e-06
learn_rate = 0.05
decay_rate = 0.01


def xor(a, b, bound):
    total, bit = 0, 1
    while bit < bound:
        total = total + ((a // bit + b // bit) % 2) * bit
        bit *= 2
    return total


def flips(here, bound):
    steps, bit = [], 1
    while bit < bound:
        steps.append(bit - 2 * bit * ((here // bit) % 2))
        bit *= 2
    return [
        here + sum(step for b, step in enumerate(steps) if (k >> b) % 2) for k in range(bound)
    ]


def sub_order(subs):
    width = subs.bit_length() - 1
    codes = [i ^ (i >> 1) for i in range(subs)]
    return [sum(((c >> b) & 1) << (width - 1 - b) for b in range(width)) for c in codes]


def prepare(groups, subs, partner, ids, master_hbm, one_hbm, two_hbm, staged, row_ids,
            master, one, two, load_sem):
    devices = groups * subs
    rows_dev, width = master.shape
    block = rows_dev // devices
    many = TILE // block
    me = lax.axis_index("grp") * subs + lax.axis_index("sub")
    loads = [
        pltpu.make_async_copy(src, dst, load_sem.at[i])
        for i, (src, dst) in enumerate([(master_hbm, master), (one_hbm, one), (two_hbm, two)])
    ]
    for load in loads:
        load.start()

    def rank_of(device):
        def seek(n, found):
            return found + jnp.where(partner[n] == device, n, 0)

        return lax.fori_loop(0, devices, seek, jnp.int32(0), unroll=8)

    my_rank = rank_of(me)
    sub_iota = lax.broadcasted_iota(jnp.int32, (TILE, LANES), 0)

    def name_rows(s, carry):
        here = jnp.zeros((TILE, LANES), jnp.int32)
        for i in range(many):
            for b in range(block):
                tensor = ids[(s * many + i) * rows_dev + my_rank * block + b]
                here = jnp.where(sub_iota == i * block + b, tensor, here)
        row_ids[pl.ds(pl.multiple_of(s * TILE, TILE), TILE), :] = here
        return carry

    lax.fori_loop(0, rows_dev // TILE, name_rows, 0)
    for load in loads:
        load.wait()

    def stage(n, carry):
        peer = partner[n]
        base = pl.multiple_of((n // many) * TILE, TILE)
        part = n % many
        for a, source in enumerate((master, one, two)):
            rows = source[pl.ds(base, TILE), :]
            piece = rows[:block]
            for i in range(1, many):
                piece = jnp.where(part == i, rows[i * block : (i + 1) * block], piece)
            staged[peer, a] = piece
        return carry

    lax.fori_loop(0, devices, stage, 0)


def kernel(groups, subs, staged, row_ids, grad_hbm,
           weights, update, first_out, second_out, ratio_out,
           grad, landed, acc_w, acc_u, sums,
           load_sem, send_sem, recv_sem, sum_send, sum_recv):
    devices = groups * subs
    rows_dev, width = grad.shape
    block = rows_dev // devices
    many = TILE // block
    halves = subs // many
    columns = width // LANES
    my_grp, my_sub = lax.axis_index("grp"), lax.axis_index("sub")
    me = my_grp * subs + my_sub
    grps, sbs = flips(my_grp, groups), flips(my_sub, subs)
    order = sub_order(subs)
    peers = [g * subs + s for s in order for g in range(groups) if g or s]

    def at(k):
        return {"grp": grps[k // subs], "sub": sbs[k % subs]}

    load = pltpu.make_async_copy(grad_hbm, grad, load_sem)
    load.start()
    barrier = pltpu.get_barrier_semaphore()
    for k in reversed(peers):
        pl.semaphore_signal(barrier, inc=1, device_id=at(k), device_id_type=MESH)
    pl.semaphore_wait(barrier, devices - 1)

    def exchange(k):
        return pltpu.make_async_remote_copy(
            src_ref=staged.at[grps[k // subs] * subs + sbs[k % subs]],
            dst_ref=landed.at[k],
            send_sem=send_sem.at[k],
            recv_sem=recv_sem.at[k],
            device_id=at(k),
            device_id_type=MESH,
        )

    def exchange_sum(k):
        return pltpu.make_async_remote_copy(
            src_ref=sums.at[0],
            dst_ref=sums.at[k],
            send_sem=sum_send.at[k],
            recv_sem=sum_recv.at[k],
            device_id=at(k),
            device_id_type=MESH,
        )

    for k in peers:
        exchange(k).start()
    landed[0] = staged[me]
    load.wait()
    acc_w[...] = jnp.zeros_like(acc_w)
    acc_u[...] = jnp.zeros_like(acc_u)
    sub_iota = lax.broadcasted_iota(jnp.int32, (TILE, LANES), 0)
    lane_iota = lax.broadcasted_iota(jnp.int32, (TILE, LANES), 1)
    scale_one = 1.0 / (1.0 - beta_one**step_count)
    scale_two = 1.0 / (1.0 - beta_two**step_count)
    within = flips(me % many, many)

    def consume(j):
        base = pl.multiple_of(xor(me // many, j, devices // many) * TILE, TILE)
        slots = [j * many + within[i] for i in range(many)]
        here = row_ids[pl.ds(base, TILE), :]
        sum_w = jnp.zeros((TILE, LANES), jnp.float32)
        sum_u = jnp.zeros((TILE, LANES), jnp.float32)
        for c in range(columns):
            cut = slice(c * LANES, (c + 1) * LANES)

            def arrived(a):
                return jnp.concatenate([landed[slot, a, :, cut] for slot in slots], axis=0)

            g = grad[pl.ds(base, TILE), cut]
            w = arrived(0)
            first = beta_one * arrived(1) + (1.0 - beta_one) * g
            second = beta_two * arrived(2) + (1.0 - beta_two) * g * g
            u = (first * scale_one) / (jnp.sqrt(second * scale_two) + adam_eps) + decay_rate * w
            first_out[pl.ds(base, TILE), cut] = first
            second_out[pl.ds(base, TILE), cut] = second
            weights[pl.ds(base, TILE), cut] = w
            update[pl.ds(base, TILE), cut] = u
            sum_w += w * w
            sum_u += u * u
        for t in range(LAYERS):
            acc_w[t] += jnp.where(here == t, sum_w, 0.0)
            acc_u[t] += jnp.where(here == t, sum_u, 0.0)

    def receive(j, carry):
        for i in range(many):
            pltpu.make_async_remote_copy(
                src_ref=staged.at[0],
                dst_ref=landed.at[j * many + i],
                send_sem=send_sem.at[j * many + i],
                recv_sem=recv_sem.at[j * many + i],
                device_id=at(1),
                device_id_type=MESH,
            ).wait_recv()
        consume(j)
        return carry

    for h in sorted(range(halves), key=lambda h: max(order.index(h * many + i) for i in range(many))):
        if h == 0:
            for i in range(1, many):
                exchange(i).wait_recv()
            consume(0)
        lax.fori_loop(1 if h == 0 else 0, groups, lambda g, c, h=h: receive(g * halves + h, c), 0)

    col_w = jnp.sum(jnp.sum(acc_w[...], axis=1), axis=1, keepdims=True)
    col_u = jnp.sum(jnp.sum(acc_u[...], axis=1), axis=1, keepdims=True)
    spread = jnp.where(lane_iota == sub_iota, col_w, 0.0) + jnp.where(
        lane_iota == sub_iota + LAYERS, col_u, 0.0
    )
    sums[0] = jnp.sum(spread, axis=0, keepdims=True)
    for k in reversed(peers):
        exchange(k).wait_send()
    for k in reversed(range(1, devices)):
        exchange_sum(k).start()
    for k in range(1, devices):
        exchange_sum(k).wait_recv()
    for k in range(1, devices):
        exchange_sum(k).wait_send()
    mine = flips(me, devices)
    total = jnp.zeros((1, LANES), jnp.float32)
    for o in range(devices):
        total = total + sums[mine[o]]
    wide = jnp.broadcast_to(total, (TILE, LANES))
    weight_sq = jnp.sum(jnp.where(lane_iota == sub_iota, wide, 0.0), axis=1, keepdims=True)
    update_sq = jnp.sum(jnp.where(lane_iota == sub_iota + LAYERS, wide, 0.0), axis=1, keepdims=True)
    ratio = learn_rate * (jnp.sqrt(weight_sq) / (jnp.sqrt(update_sq) + trust_eps))
    ratio_out[...] = jnp.broadcast_to(ratio, (TILE, LANES))


def finish(ratio_ref, row_ids, weights, update, first, second,
           fresh_hbm, first_hbm, second_hbm, fresh, fresh_sem, moment_sem):
    rows_dev, width = weights.shape
    columns = width // LANES
    moments = [
        pltpu.make_async_copy(first, first_hbm, moment_sem.at[0]),
        pltpu.make_async_copy(second, second_hbm, moment_sem.at[1]),
    ]
    for move in moments:
        move.start()
    ratio = ratio_ref[...]
    span = rows_dev // PIECES
    moves = []
    for p in range(PIECES):

        def step_rows(s, carry):
            base = pl.multiple_of(p * span + s * TILE, TILE)
            here = row_ids[pl.ds(base, TILE), :]
            step = jnp.zeros((TILE, LANES), jnp.float32)
            for t in range(LAYERS):
                step = jnp.where(here == t, jnp.broadcast_to(ratio[t : t + 1], (TILE, LANES)), step)
            for c in range(columns):
                cut = slice(c * LANES, (c + 1) * LANES)
                rows = pl.ds(base, TILE)
                fresh[rows, cut] = weights[rows, cut] - step * update[rows, cut]
            return carry

        lax.fori_loop(0, span // TILE, step_rows, 0)
        rows = pl.ds(p * span, span)
        moves.append(pltpu.make_async_copy(fresh.at[rows], fresh_hbm.at[rows], fresh_sem.at[p]))
        if p:
            moves[p - 1].start()
    moves[-1].start()
    for move in moves + moments:
        move.wait()


def local(groups, subs, master, moment_one, moment_two, gradient, partner, tensor_of_row):
    rows_dev, width = master.shape
    devices = groups * subs
    block = rows_dev // devices
    whole = jax.ShapeDtypeStruct((rows_dev, width), jnp.float32)
    vmem = pl.BlockSpec(memory_space=pltpu.VMEM)
    smem = pl.BlockSpec(memory_space=pltpu.SMEM)
    hbm = pl.BlockSpec(memory_space=pltpu.HBM)
    slots = (devices, 3, block, width)
    staged, row_ids = pl.pallas_call(
        functools.partial(prepare, groups, subs),
        out_shape=(
            pltpu.VMEM(slots, jnp.float32),
            pltpu.VMEM((rows_dev, LANES), jnp.int32),
        ),
        in_specs=[smem, smem, hbm, hbm, hbm],
        out_specs=(vmem, vmem),
        scratch_shapes=[pltpu.VMEM((rows_dev, width), jnp.float32)] * 3
        + [pltpu.SemaphoreType.DMA((3,))],
        compiler_params=pltpu.CompilerParams(vmem_limit_bytes=54 * 1024 * 1024),
    )(partner, tensor_of_row, master, moment_one, moment_two)
    weights, update, first, second, ratio = pl.pallas_call(
        functools.partial(kernel, groups, subs),
        out_shape=(whole, whole, whole, whole, jax.ShapeDtypeStruct((LAYERS, LANES), jnp.float32)),
        in_specs=[vmem, vmem, hbm],
        out_specs=(vmem, vmem, vmem, vmem, vmem),
        scratch_shapes=[
            pltpu.VMEM((rows_dev, width), jnp.float32),
            pltpu.VMEM(slots, jnp.float32),
            pltpu.VMEM((LAYERS, TILE, LANES), jnp.float32),
            pltpu.VMEM((LAYERS, TILE, LANES), jnp.float32),
            pltpu.VMEM((devices, 1, LANES), jnp.float32),
            pltpu.SemaphoreType.DMA,
            pltpu.SemaphoreType.DMA((devices,)),
            pltpu.SemaphoreType.DMA((devices,)),
            pltpu.SemaphoreType.DMA((devices,)),
            pltpu.SemaphoreType.DMA((devices,)),
        ],
        compiler_params=pltpu.CompilerParams(
            collective_id=0, has_side_effects=True, vmem_limit_bytes=32 * 1024 * 1024
        ),
    )(staged, row_ids, gradient)
    return pl.pallas_call(
        finish,
        out_shape=(whole, whole, whole),
        in_specs=[vmem] * 6,
        out_specs=(hbm, hbm, hbm),
        scratch_shapes=[
            pltpu.VMEM((rows_dev, width), jnp.float32),
            pltpu.SemaphoreType.DMA((PIECES,)),
            pltpu.SemaphoreType.DMA((2,)),
        ],
        compiler_params=pltpu.CompilerParams(vmem_limit_bytes=32 * 1024 * 1024),
    )(ratio, row_ids, weights, update, first, second)


def solution(mesh):
    rows = P(("grp", "sub"), None)
    return jax.shard_map(
        functools.partial(local, mesh.shape["grp"], mesh.shape["sub"]),
        mesh=mesh,
        in_specs=(rows, rows, rows, rows, P(), P()),
        out_specs=(rows, rows, rows),
        check_vma=False,
    )
```

time: 158 us -> 142 us (0.90)
  local copies, waits for them, and re-layouts: 9.69 us -> 0.01 us
  Pallas kernels: 147 us -> 141 us
    pallas_call x1, Pallas kernels: 145 us -> 134 us  [local(): pl.pallas_call(functools.partial(kernel, groups, subs), out_shape=(whole,...]
    unnamed x15 -> x2, local copies, waits for them, and re-layouts: 9.69 us -> 0.01 us
    pallas_call x1 -> x2, Pallas kernels: 2.7 us -> 7.42 us  [the longest x1 4.95 us: local(): pl.pallas_call(functools.partial(prepare, groups, subs), out_shape=(pltpu...]
where the time goes in v2:
time: 142 us
  Pallas kernels  141 us (99%)
    pallas_call x1, Pallas kernels, local(): pl.pallas_call(functools.partial(kernel, groups, subs), out_shape=(whole,...  134 us
    pallas_call x1, Pallas kernels, local(): pl.pallas_call(functools.partial(prepare, groups, subs), out_shape=(pltpu...  4.95 us

profile of v2, /device:TPU:0, one launch (start us, length us, event | category | flops | bytes accessed | tf_op | source)
XLA Modules:
  0.0 142.0 jit_solution(290142063068642372)
XLA Ops:
  0.6 0.0 copy-start
  0.6 4.9 %shard_map.85 = (f32[32,3,4,3584]{3,2,1,0:T(4,128)S(1)}, s32[128,128]{1,0:T(8,128)S(1)}) custom-call(s32[32]{0:T(128)} %partner.1, s32[4096]{0:T(1024)} %ids.1, f32[128,3584]{1,0:T(8,128)} %master_hbm.1, f32[128,3584]{1,0:T(8,128)} %one_hbm.1, f32[128,3584]{1,0:T(8,128)} %two_hbm.1), custom_call_target="tpu_custom_call" | custom-call | tf_op jit(solution)/shard_map/pallas_call | solution.py:276
  5.6 0.0 copy-done
  5.6 134.0 %shard_map.86 = (f32[128,3584]{1,0:T(8,128)S(1)}, f32[128,3584]{1,0:T(8,128)S(1)}, f32[128,3584]{1,0:T(8,128)S(1)}, f32[128,3584]{1,0:T(8,128)S(1)}, f32[8,128]{1,0:T(8,128)S(1)}) custom-call(f32[32,3,4,3584]{3,2,1,0:T(4,128)S(1)} %get-tuple-element.10.staged, s32[128,128]{1,0:T(8,128)S(1)} %get-tuple-element.11.row_ids, f32[128,3584]{1,0:T(8,128)S(1)} %copy-done), custom_call_target="tpu_custom_call" | custom-call | tf_op jit(solution)/shard_map/pallas_call | solution.py:288
  139.6 2.5 %shard_map.87 = (f32[128,3584]{1,0:T(8,128)}, f32[128,3584]{1,0:T(8,128)}, f32[128,3584]{1,0:T(8,128)}) custom-call(f32[8,128]{1,0:T(8,128)S(1)} %get-tuple-element.12.ratio_ref, s32[128,128]{1,0:T(8,128)S(1)} %get-tuple-element.11.row_ids, f32[128,3584]{1,0:T(8,128)S(1)} %get-tuple-element.13.weights, f32[128,3584]{1,0:T(8,128)S(1)} %get-tuple-element.14.update, ...), custom_call_target="tpu_custom_call" | custom-call | tf_op jit(solution)/shard_map/pallas_call | solution.py:309
Async XLA Ops:
  0.6 5.0 %copy-start = (f32[128,3584]{1,0:T(8,128)S(1)}, f32[128,3584]{1,0:T(8,128)}, u32[]{:S(2)}) copy-start(f32[128,3584]{1,0:T(8,128)} %grad_hbm.1) | copy-start | bytes 5505028

commit v3 on v2

--- a/solution.py
+++ b/solution.py
@@ -69,32 +69,26 @@
     my_rank = rank_of(me)
     sub_iota = lax.broadcasted_iota(jnp.int32, (TILE, LANES), 0)
 
-    def name_rows(s, carry):
+    def name_rows(s):
         here = jnp.zeros((TILE, LANES), jnp.int32)
         for i in range(many):
             for b in range(block):
                 tensor = ids[(s * many + i) * rows_dev + my_rank * block + b]
                 here = jnp.where(sub_iota == i * block + b, tensor, here)
         row_ids[pl.ds(pl.multiple_of(s * TILE, TILE), TILE), :] = here
-        return carry
-
-    lax.fori_loop(0, rows_dev // TILE, name_rows, 0)
-    for load in loads:
-        load.wait()
-
-    def stage(n, carry):
-        peer = partner[n]
-        base = pl.multiple_of((n // many) * TILE, TILE)
-        part = n % many
-        for a, source in enumerate((master, one, two)):
-            rows = source[pl.ds(base, TILE), :]
-            piece = rows[:block]
-            for i in range(1, many):
-                piece = jnp.where(part == i, rows[i * block : (i + 1) * block], piece)
-            staged[peer, a] = piece
-        return carry
-
-    lax.fori_loop(0, devices, stage, 0)
+
+    for a, source in enumerate((master, one, two)):
+        loads[a].wait()
+
+        def stage(s, carry, a=a, source=source):
+            rows = source[pl.ds(pl.multiple_of(s * TILE, TILE), TILE), :]
+            for i in range(many):
+                staged[partner[s * many + i], a] = rows[i * block : (i + 1) * block]
+            if a == 0:
+                name_rows(s)
+            return carry
+
+        lax.fori_loop(0, rows_dev // TILE, stage, 0)
 
 
 def kernel(groups, subs, staged, row_ids, grad_hbm,
@@ -209,9 +203,9 @@
     )
     sums[0] = jnp.sum(spread, axis=0, keepdims=True)
     for k in reversed(peers):
+        exchange_sum(k).start()
+    for k in peers:
         exchange(k).wait_send()
-    for k in reversed(range(1, devices)):
-        exchange_sum(k).start()
     for k in range(1, devices):
         exchange_sum(k).wait_recv()
     for k in range(1, devices):

time: 142 us -> 141 us (level)
  no operation moved by 1% of the time
where the time goes in v3:
time: 141 us
  Pallas kernels  140 us (99%)
    pallas_call x1, Pallas kernels, local(): pl.pallas_call(functools.partial(kernel, groups, subs), out_shape=(whole,...  134 us
    pallas_call x1, Pallas kernels, local(): pl.pallas_call(functools.partial(prepare, groups, subs), out_shape=(pltpu...  3.9 us

profile of v3, /device:TPU:0, one launch (start us, length us, event | category | flops | bytes accessed | tf_op | source)
XLA Modules:
  0.0 141.0 jit_solution(8903337704589550161)
XLA Ops:
  0.6 0.0 copy-start
  0.6 3.9 %shard_map.85 = (f32[32,3,4,3584]{3,2,1,0:T(4,128)S(1)}, s32[128,128]{1,0:T(8,128)S(1)}) custom-call(s32[32]{0:T(128)} %partner.1, s32[4096]{0:T(1024)} %ids.1, f32[128,3584]{1,0:T(8,128)} %master_hbm.1, f32[128,3584]{1,0:T(8,128)} %one_hbm.1, f32[128,3584]{1,0:T(8,128)} %two_hbm.1), custom_call_target="tpu_custom_call" | custom-call | tf_op jit(solution)/shard_map/pallas_call | solution.py:270
  4.6 0.0 copy-done
  4.6 133.9 %shard_map.86 = (f32[128,3584]{1,0:T(8,128)S(1)}, f32[128,3584]{1,0:T(8,128)S(1)}, f32[128,3584]{1,0:T(8,128)S(1)}, f32[128,3584]{1,0:T(8,128)S(1)}, f32[8,128]{1,0:T(8,128)S(1)}) custom-call(f32[32,3,4,3584]{3,2,1,0:T(4,128)S(1)} %get-tuple-element.10.staged, s32[128,128]{1,0:T(8,128)S(1)} %get-tuple-element.11.row_ids, f32[128,3584]{1,0:T(8,128)S(1)} %copy-done), custom_call_target="tpu_custom_call" | custom-call | tf_op jit(solution)/shard_map/pallas_call | solution.py:282
  138.5 2.5 %shard_map.87 = (f32[128,3584]{1,0:T(8,128)}, f32[128,3584]{1,0:T(8,128)}, f32[128,3584]{1,0:T(8,128)}) custom-call(f32[8,128]{1,0:T(8,128)S(1)} %get-tuple-element.12.ratio_ref, s32[128,128]{1,0:T(8,128)S(1)} %get-tuple-element.11.row_ids, f32[128,3584]{1,0:T(8,128)S(1)} %get-tuple-element.13.weights, f32[128,3584]{1,0:T(8,128)S(1)} %get-tuple-element.14.update, ...), custom_call_target="tpu_custom_call" | custom-call | tf_op jit(solution)/shard_map/pallas_call | solution.py:303
Async XLA Ops:
  0.6 3.9 %copy-start = (f32[128,3584]{1,0:T(8,128)S(1)}, f32[128,3584]{1,0:T(8,128)}, u32[]{:S(2)}) copy-start(f32[128,3584]{1,0:T(8,128)} %grad_hbm.1) | copy-start | bytes 5505028
